TPU v7x, 32 devices: a whole 2x2x4 slice. The times are simulated.
32 devices in a mesh: tp: 4 (over z), pp: 8 (over y, x, core).
Axes of the slice: x: 2, y: 2, z: 4, core: 2. Of those that a mesh axis runs over, the one named last changes fastest.
Arguments:
- tokens: bfloat16 [8192, 8192], P('pp', 'tp'), may hold values from -60 to 60
- norm_gain: bfloat16 [8192], P('tp'), may hold values from 0.099609375 to 1.8984375
- weights_gen: bfloat16 [8, 1280, 8192], P('tp', None, 'pp'), may hold values from -2 to 2
- segment_ids: int32 [8, 1024], P('pp'), may hold values from 0 to 15, never falling along the last dimension, each value on 1 to 512 neighbouring positions
Outputs:
- weights_rows: bfloat16 [8, 1280, 8192], P('tp', 'pp')
- attended: bfloat16 [8192, 8192], P('pp', 'tp')
Inputs may be any that keep to these rules, and one draw needn't show every extreme that they name: `segment_ids`: ids never fall along a block; every sequence has 1 to 512 tokens and lies in one block.
All inputs are finite; a program needn't handle non-finite values.
Results may differ from a plain program's by a relative error of at most 0.0075.
Values may be sent and summed in bfloat16 or wider, within the bound.
A program may use at most 192 MiB of HBM per device.

v0:
```python
import math

import jax
import jax.numpy as jnp
from jax import lax
from jax.sharding import PartitionSpec as P

DH = 128
GROUP = 8


rope_base = 500000.0


def rotary(values, positions):
    half = values.shape[-1] // 2
    freq = jnp.exp(
        jnp.arange(half, dtype=jnp.float32) * (-2.0 * math.log(rope_base) / values.shape[-1])
    )
    angle = positions.astype(jnp.float32)[:, None] * freq[None, :]
    cosine = jnp.cos(angle)
    sine = jnp.sin(angle)
    extra = values.ndim - 2
    cosine = cosine.reshape(cosine.shape[:1] + (1,) * extra + cosine.shape[1:])
    sine = sine.reshape(sine.shape[:1] + (1,) * extra + sine.shape[1:])
    first = values[..., :half]
    second = values[..., half:]
    return jnp.concatenate(
        [first * cosine - second * sine, second * cosine + first * sine], axis=-1
    )


def shards(tokens, norm_gain, weights_gen, segment_ids):
    weights_rows = lax.all_to_all(weights_gen, "pp", split_axis=1, concat_axis=2, tiled=True)
    gathered, gain = (
        lax.all_gather(tokens, "tp", axis=1, tiled=True),
        lax.all_gather(norm_gain, "tp", axis=0, tiled=True),
    )
    floats = gathered.astype(jnp.float32)
    square = jnp.mean(floats * floats, axis=-1, keepdims=True)
    normed = (floats * lax.rsqrt(square + 1e-05) * gain.astype(jnp.float32)).astype(jnp.bfloat16)
    count = normed.shape[0]
    groups = weights_gen.shape[0]
    mixed = jnp.einsum(
        "td,grd->tgr",
        normed,
        lax.all_gather(weights_rows, "pp", axis=1, tiled=True),
        preferred_element_type=jnp.float32,
    )
    mixed = mixed.reshape(count, groups, GROUP + 2, DH)
    seg = segment_ids[0]
    order = jnp.arange(count, dtype=jnp.int32)
    start_index = jnp.sum((seg[None, :] < seg[:, None]).astype(jnp.int32), axis=1)
    positions = order - start_index
    query = rotary(mixed[:, :, :GROUP, :], positions).astype(jnp.bfloat16)
    key_heads = rotary(mixed[:, :, GROUP, :], positions).astype(jnp.bfloat16)
    value_heads = mixed[:, :, GROUP + 1, :].astype(jnp.bfloat16)
    score = jnp.einsum("tgjd,sgd->gjts", query, key_heads, preferred_element_type=jnp.float32) * (
        1.0 / math.sqrt(DH)
    )
    allowed = (seg[:, None] == seg[None, :]) & (order[:, None] >= order[None, :])
    score = jnp.where(allowed[None, None], score, -1e30)
    top = jnp.max(score, axis=-1, keepdims=True)
    expo = jnp.where(allowed[None, None], jnp.exp(score - top), 0.0)
    prob = (expo / jnp.sum(expo, axis=-1, keepdims=True)).astype(jnp.bfloat16)
    output = jnp.einsum("gjts,sgd->tgjd", prob, value_heads, preferred_element_type=jnp.float32)
    attended = output.astype(jnp.bfloat16).reshape(count, groups * GROUP * DH)
    return (weights_rows, attended)


def solution(mesh):
    in_specs = (P("pp", "tp"), P("tp"), P("tp", None, "pp"), P("pp", None))
    out_specs = (P("tp", "pp", None), P("pp", "tp"))
    return jax.shard_map(shards, mesh=mesh, in_specs=in_specs, out_specs=out_specs, check_vma=False)
```

profile of v0, /device:TPU:0, one launch (start us, length us, event | category | flops | bytes accessed | tf_op | source)
XLA Modules:
  0.0 658.1 jit_solution(8889944450149644430)
XLA Ops:
  7.2 0.0 all-gather.3.cloned.1.call-start
  7.2 0.7 all-gather.3.cloned.1.call-update
  7.9 0.0 all-gather.5.cloned.1.call-start
  7.9 9.4 %copy.21 = bf16[2,1280,1024]{2,0,1:T(2,128)(2,1)S(1)} copy(bf16[2,1280,1024]{2,1,0:T(8,128)(2,1)} %param.6) | data formatting | bytes 10485760 | tf_op args[2]
  17.4 65.3 %all_to_all.18 = bf16[2,1280,1024]{2,0,1:T(2,128)(2,1)S(1)} all-to-all(bf16[2,1280,1024]{2,0,1:T(2,128)(2,1)S(1)} %copy.21), channel_id=1, replica_groups=mesh['tp'=4,'pp'=8] {'pp'}, dimensions={1} | all-to-all | bytes 10485760 | tf_op jit(solution)/shard_map/all_to_all | solution.py:34
  82.6 5.2 copy.43
  87.8 0.0 copy-start.2
  87.8 0.0 copy-start.1
  87.8 8.9 %all_to_all.16 = bf16[2,160,8192]{2,1,0:T(8,128)(2,1)} reshape(bf16[2,160,8,1024]{3,2,1,0:T(8,128)(2,1)} %bitcast.49) | data formatting | bytes 10485760 | tf_op jit(solution)/shard_map/all_to_all | solution.py:34
  96.8 0.0 all-gather.5.cloned.1.call-update
  96.8 0.0 copy-done.2
  96.8 24.4 %all_gather.10 = bf16[8192]{0:T(1024)(128)(2,1)S(1)} all-gather(bf16[2048]{0:T(1024)(128)(2,1)S(1)} %copy-done.2), channel_id=1, replica_groups=mesh['tp'=4,'pp'=8] {'tp'}, dimensions={0}, use_global_device_ids=true | all-gather | bytes 20480 | tf_op jit(solution)/shard_map/all_gather | solution.py:37
  121.2 0.0 copy-done.1
  121.2 0.5 convert_reduce_fusion
  121.7 1.9 multiply_cosine_fusion
  123.6 1.6 fusion.16
  125.1 174.1 %all-gather.3.cloned.1.call-done = bf16[1024,8192]{1,0:T(8,128)(2,1)} async-done(((bf16[1024,2048]{1,0:T(8,128)(2,1)}), bf16[1024,8192]{1,0:T(8,128)(2,1)}) %all-gather.3.cloned.1.call-update) | async-done | bytes 16777232 | tf_op jit(solution)/shard_map/all_gather | solution.py:36
  299.3 7.2 %fusion.2 = f32[1024]{0:T(1024)S(1)} fusion(bf16[1024,8192]{1,0:T(8,128)(2,1)} %all-gather.3.cloned.1.call-done), kind=kLoop, calls=%fused_computation.7 | loop fusion | flops 25164800 | bytes 16781312 | tf_op jit(solution)/shard_map/reduce_sum | solution.py:40
  306.5 189.8 %all-gather.5.cloned.1.call-done = bf16[2,1280,8192]{2,1,0:T(8,128)(2,1)} async-done(((bf16[2,160,8192]{2,1,0:T(8,128)(2,1)}), bf16[2,1280,8192]{2,1,0:T(8,128)(2,1)}) %all-gather.5.cloned.1.call-update) | async-done | bytes 41943056 | tf_op jit(solution)/shard_map/all_gather | solution.py:47
  496.3 54.2 %fusion.10 = f32[1024,2,1280]{0,2,1:T(8,128)} fusion(bf16[2,1280,8192]{2,1,0:T(8,128)(2,1)} %all-gather.5.cloned.1.call-done, bf16[1024,8192]{1,0:T(8,128)(2,1)} %all-gather.3.cloned.1.call-done, f32[8192]{0:T(1024)S(1)} %convert_element_type.36, f32[1024]{0:T(1024)S(1)} %add_rsqrt_fusion), kind=kOutput, calls=%fused_computation.15 | convolution fusion | flops 42983227392 | bytes 69242880 | tf_op jit(solution)/shard_map/td,grd->tgr/dot_general | solution.py:44
  550.5 1.3 slice.29
  551.8 8.5 %fusion.27 = (f32[1024,2,8,64]{0,3,2,1:T(8,128)}, f32[1024,2,8,64]{0,3,2,1:T(8,128)}) fusion(f32[1024,2,10,128]{0,3,2,1:T(8,128)} %bitcast.52), kind=kLoop, calls=%fused_computation.42 | loop fusion | bytes 16777216 | tf_op jit(solution)/shard_map/slice | solution.py:27
  560.2 0.3 copy.34
  560.5 6.9 %copy.36 = f32[1024,2,8,64]{3,0,2,1:T(8,128)} copy(f32[1024,2,8,64]{0,3,2,1:T(8,128)} %get-tuple-element.10) | data formatting | bytes 8388608
  567.5 6.9 %copy.35 = f32[1024,2,8,64]{3,0,2,1:T(8,128)} copy(f32[1024,2,8,64]{0,3,2,1:T(8,128)} %get-tuple-element.11) | data formatting | bytes 8388608
  574.3 0.4 subtract_convert_fusion.1
  574.7 0.0 copy-start
  574.8 9.6 %subtract_convert_fusion = (bf16[1024,2,8,64]{3,0,2,1:T(8,128)(2,1)}, bf16[1024,2,8,64]{3,0,2,1:T(8,128)(2,1)}) fusion(f32[1024,2,8,64]{3,0,2,1:T(8,128)} %copy.36, f32[1024,2,8,64]{3,0,2,1:T(8,128)} %copy.35, f32[1024,64]{1,0:T(8,128)S(1)} %get-tuple-element.15, f32[1024,64]{1,0:T(8,128)S(1)} %get-tuple-element.14), kind=kLoop, calls=%fused_computation.19 | loop fusion | flops 8388608 | bytes 13107200 | tf_op jit(solution)/shard_map/convert
  584.4 0.0 copy-done
  584.4 36.3 %fusion.28 = (f32[2,8,1024]{2,1,0:T(8,128)S(1)}, f32[2,8,1024,1024]{2,3,1,0:T(8,128)}) fusion(pred[1024,1024]{0,1:T(8,128)(4,1)S(1)} %copy-done, bf16[1024,2,8,64]{3,0,2,1:T(8,128)(2,1)} %get-tuple-element.9, bf16[1024,2,8,64]{3,0,2,1:T(8,128)(2,1)} %get-tuple-element.8, bf16[1024,2,64]{2,0,1:T(8,128)(2,1)S(1)} %get-tuple-element.13, ...), kind=kOutput, calls=%fused_computation.43 | convolution fusion | flops 4388291584 | bytes 72941568 | tf_op jit(solution)/shard_map/sub | solution.py:64
  620.7 24.1 %fusion.17 = bf16[2,128,8,1024]{3,1,2,0:T(8,128)(2,1)} fusion(f32[2,8,1024,1024]{2,3,1,0:T(8,128)} %get-tuple-element.17, f32[2,8,1024]{2,1,0:T(8,128)S(1)} %get-tuple-element.16, f32[1024,2,10,128]{0,3,2,1:T(8,128)} %bitcast.53), kind=kOutput, calls=%fused_computation.26 | convolution fusion | flops 4330618880 | bytes 71892992 | tf_op jit(solution)/shard_map/gjts,sgd->tgjd/dot_general | solution.py:66
  644.8 6.4 copy.29
  (4 shorter events, 0.0 us)
Async XLA Ops:
  7.2 292.1 %all-gather.3.cloned.1.call-start = ((), (), s32[]{:S(2)}) async-start(), calls=%async_computation.1 | async-start | bytes 20971520 | tf_op jit(solution)/shard_map/all_gather | solution.py:36
  7.9 488.4 %all-gather.5.cloned.1.call-start = ((), (), s32[]{:S(2)}) async-start(), calls=%async_computation.2 | async-start | bytes 47185920 | tf_op jit(solution)/shard_map/all_gather | solution.py:47
  87.8 8.9 %copy-start.2 = (bf16[2048]{0:T(1024)(128)(2,1)S(1)}, bf16[2048]{0:T(1024)(128)(2,1)}, u32[]{:S(2)}) copy-start(bf16[2048]{0:T(1024)(128)(2,1)} %param.5) | copy-start | bytes 12292
  87.8 33.3 %copy-start.1 = (s32[1,1024]{1,0:T(1,128)S(1)}, s32[1,1024]{1,0:T(1,128)}, u32[]{:S(2)}) copy-start(s32[1,1024]{1,0:T(1,128)} %param.7) | copy-start | bytes 12292
  574.7 9.7 %copy-start = (pred[1024,1024]{0,1:T(8,128)(4,1)S(1)}, pred[1024,1024]{0,1:T(8,128)(4,1)}, u32[]{:S(2)}) copy-start(pred[1024,1024]{0,1:T(8,128)(4,1)} %fusion.16) | copy-start | bytes 3145732
Sparse Core Ops, SparseCore 0:
  9.5 289.6 all-gather.2
  301.7 194.4 all-gather.4
where the time goes:
time: 659 us; the launch traced here: 658 us
  waiting for transfers between devices  365 us (55%)
  matrix products  115 us (17%)
  blocking collectives  89.6 us (14%)
  local copies, waits for them, and re-layouts  53.8 us (8%)
  other arithmetic  21.2 us (3%)
  between operations  14.1 us (2%)
    all_gather x1, waiting for transfers between devices, shards(): lax.all_gather(weights_rows, 'pp', axis=1, tiled=True)  190 us
    all_gather x1, waiting for transfers between devices, shards(): lax.all_gather(tokens, 'tp', axis=1, tiled=True)  174 us
    all_to_all x1, blocking collectives, shards(): lax.all_to_all(weights_gen, 'pp', split_axis=1, concat_axis=2, tiled=True)  65.3 us
    dot_general x1, matrix products, shards(): jnp.einsum('td,grd->tgr', normed, lax.all_gather(weights_rows, 'pp', axis...  54.2 us
    sub x1, matrix products, shards(): expo = jnp.where(allowed[None, None], jnp.exp(score - top), 0.0)  36.3 us
    unnamed x11, local copies, waits for them, and re-layouts  29.9 us
    all_gather x1, blocking collectives, shards(): lax.all_gather(norm_gain, 'tp', axis=0, tiled=True)  24.4 us
    dot_general x1, matrix products, shards(): jnp.einsum('gjts,sgd->tgjd', prob, value_heads, preferred_element_type=jn...  24.1 us
  transfers between devices with their start and end apart: 2, of which 2 were waited for; matrix products, arithmetic and copies ran while one was open for 4% of the time, Pallas kernels for 0%

commit v1 on v0

v1 whole, which is shorter than its diff:
```python
import functools
import math

import jax
import jax.numpy as jnp
from jax import lax
from jax.sharding import PartitionSpec as P


DH = 128
GROUP = 8


rope_base = 500000.0


def rotary(values, positions):
    half = values.shape[-1] // 2
    freq = jnp.exp(
        jnp.arange(half, dtype=jnp.float32) * (-2.0 * math.log(rope_base) / values.shape[-1])
    )
    angle = positions.astype(jnp.float32)[:, None] * freq[None, :]
    cosine = jnp.cos(angle)
    sine = jnp.sin(angle)
    extra = values.ndim - 2
    cosine = cosine.reshape(cosine.shape[:1] + (1,) * extra + cosine.shape[1:])
    sine = sine.reshape(sine.shape[:1] + (1,) * extra + sine.shape[1:])
    first = values[..., :half]
    second = values[..., half:]
    return jnp.concatenate(
        [first * cosine - second * sine, second * cosine + first * sine], axis=-1
    )


MAX_SEQUENCE = 512


def layer(size, *arguments):
    return shards(size, *arguments)


def shards(size, tokens, norm_gain, weights_gen, segment_ids):
    pieces = lax.all_gather(weights_gen, "pp", axis=0)
    parts, groups, rows, width = pieces.shape
    kept = rows // parts
    own = lax.dynamic_slice_in_dim(pieces, lax.axis_index("pp") * kept, kept, axis=2)
    weights_rows = own.transpose(1, 2, 0, 3).reshape(groups, kept, parts * width)

    count, local = tokens.shape
    floats = tokens.astype(jnp.float32)
    squares = lax.all_gather(jnp.sum(floats * floats, axis=-1), "tp", axis=0)
    square = jnp.sum(squares, axis=0)[:, None] * (1.0 / (size * local))
    normed = (floats * lax.rsqrt(square + 1e-05) * norm_gain.astype(jnp.float32)).astype(jnp.bfloat16)

    me = lax.axis_index("tp")
    per = local // width

    def added(total, block, owner):
        owner = jnp.clip(owner, 0, size - 1)
        for p in range(per):
            piece = lax.dynamic_index_in_dim(pieces, owner * per + p, axis=0, keepdims=False)
            term = jnp.einsum(
                "td,grd->tgr",
                block[:, p * width : (p + 1) * width],
                piece,
                preferred_element_type=jnp.float32,
            )
            total = lax.optimization_barrier(term if total is None else total + term)
        return total

    up = down = normed
    mixed = added(None, normed, me)
    for step in range(1, size):
        up = lax.ppermute(up, "tp", [(i, i + 1) for i in range(step - 1, size - 1)])
        down = lax.ppermute(down, "tp", [(i + 1, i) for i in range(size - step)])
        if 2 * step >= size:
            below = me >= step
            mixed = added(mixed, jnp.where(below, up, down), jnp.where(below, me - step, me + step))
        else:
            mixed = added(mixed, up, me - step)
            mixed = added(mixed, down, me + step)
    mixed = mixed.reshape(count, groups, GROUP + 2, DH)
    seg = segment_ids[0]
    order = jnp.arange(count, dtype=jnp.int32)
    start_index = jnp.sum((seg[None, :] < seg[:, None]).astype(jnp.int32), axis=1)
    positions = order - start_index
    query = rotary(mixed[:, :, :GROUP, :], positions).astype(jnp.bfloat16)
    key_heads = rotary(mixed[:, :, GROUP, :], positions).astype(jnp.bfloat16)
    value_heads = mixed[:, :, GROUP + 1, :].astype(jnp.bfloat16)
    chunk = count // 4
    outputs = []
    for c in range(4):
        low, high = c * chunk, (c + 1) * chunk
        first = max(0, (low - MAX_SEQUENCE + 1) // chunk * chunk)
        score = jnp.einsum(
            "tgjd,sgd->gjts",
            query[low:high],
            key_heads[first:high],
            preferred_element_type=jnp.float32,
        ) * (1.0 / math.sqrt(DH))
        allowed = (seg[low:high, None] == seg[None, first:high]) & (
            order[low:high, None] >= order[None, first:high]
        )
        score = jnp.where(allowed[None, None], score, -1e30)
        top = jnp.max(score, axis=-1, keepdims=True)
        expo = jnp.where(allowed[None, None], jnp.exp(score - top), 0.0)
        prob = (expo / jnp.sum(expo, axis=-1, keepdims=True)).astype(jnp.bfloat16)
        output = jnp.einsum(
            "gjts,sgd->tgjd", prob, value_heads[first:high], preferred_element_type=jnp.float32
        )
        outputs.append(output.astype(jnp.bfloat16).reshape(chunk, groups * GROUP * DH))
    attended = jnp.concatenate(outputs, axis=0)
    return (weights_rows, attended)


def solution(mesh):
    in_specs = (P("pp", "tp"), P("tp"), P("tp", None, "pp"), P("pp", None))
    out_specs = (P("tp", "pp", None), P("pp", "tp"))
    return jax.shard_map(
        functools.partial(layer, mesh.shape["tp"]),
        mesh=mesh,
        in_specs=in_specs,
        out_specs=out_specs,
        check_vma=False,
    )
```

time: 659 us -> 602 us (0.914)
  waiting for transfers between devices: 365 us -> 254 us
  blocking collectives: 89.6 us -> 14.9 us
  other arithmetic: 21.2 us -> 80.3 us
  matrix products: 115 us -> 165 us
  starting transfers between devices: 0.08 us -> 13 us
    all_gather x2 -> x1, waiting for transfers between devices: 364 us -> 0.01 us  [shards(): pieces = lax.all_gather(weights_gen, 'pp', axis=0)]
    ppermute x0 -> x6, waiting for transfers between devices: none -> 253 us  [the longest x3 167 us: shards(): down = lax.ppermute(down, 'tp', [(i + 1, i) for i in range(size - step)])]
    all_to_all x1 -> x0, blocking collectives: 65.3 us -> none  [shards(): lax.all_to_all(weights_gen, 'pp', split_axis=1, concat_axis=2, tiled=True)]
    dot_general x2 -> x16, matrix products: 78.4 us -> 142 us  [the longest x10 119 us: added(): jnp.einsum('td,grd->tgr', block[:, p * width:(p + 1) * width], piece, pre...]
    add x0 -> x3, other arithmetic: none -> 36.4 us  [added(): total = lax.optimization_barrier(term if total is None else total + term)]
    all_to_all x2 -> x0, local copies, waits for them, and re-layouts: 14.1 us -> none  [shards(): lax.all_to_all(weights_gen, 'pp', split_axis=1, concat_axis=2, tiled=True)]
    sub x1 -> x2, matrix products: 36.3 us -> 23 us  [shards(): expo = jnp.where(allowed[None, None], jnp.exp(score - top), 0.0)]
    ppermute x0 -> x6, starting transfers between devices: none -> 13 us  [the longest x3 9.15 us: shards(): up = lax.ppermute(up, 'tp', [(i, i + 1) for i in range(step - 1, size - 1)])]
  transfers between devices with their start and end apart: 2 -> 7, of which waited for: 2 -> 4; matrix products, arithmetic and copies ran while one was open for 4% -> 4% of each run, Pallas kernels for 0% -> 0%
where the time goes in v1:
time: 602 us; the launch traced here: 597 us
  waiting for transfers between devices  254 us (42%)
  matrix products  165 us (27%)
  other arithmetic  80.3 us (13%)
  local copies, waits for them, and re-layouts  54.9 us (9%)
  between operations  15 us (2%)
  blocking collectives  14.9 us (2%)
  starting transfers between devices  13 us (2%)
    ppermute x3, waiting for transfers between devices, shards(): down = lax.ppermute(down, 'tp', [(i + 1, i) for i in range(size - step)])  167 us
    dot_general x10, matrix products, added(): jnp.einsum('td,grd->tgr', block[:, p * width:(p + 1) * width], piece, pre...  119 us
    ppermute x3, waiting for transfers between devices, shards(): up = lax.ppermute(up, 'tp', [(i, i + 1) for i in range(step - 1, size - 1)])  85.9 us
    add x3, other arithmetic, added(): total = lax.optimization_barrier(term if total is None else total + term)  36.4 us
    sub x2, matrix products, shards(): expo = jnp.where(allowed[None, None], jnp.exp(score - top), 0.0)  23 us
    unnamed x42, local copies, waits for them, and re-layouts  22 us
    dot_general x4, matrix products, shards(): jnp.einsum('gjts,sgd->tgjd', prob, value_heads[first:high], preferred_ele...  17.6 us
    all_gather x1, blocking collectives, shards(): squares = lax.all_gather(jnp.sum(floats * floats, axis=-1), 'tp', axis=0)  14.9 us
  transfers between devices with their start and end apart: 7, of which 4 were waited for; matrix products, arithmetic and copies ran while one was open for 4% of the time, Pallas kernels for 0%

profile of v1, /device:TPU:0, one launch (start us, length us, event | category | flops | bytes accessed | tf_op | source)
XLA Modules:
  0.0 596.8 jit_solution(13705863816053863894)
XLA Ops:
  11.0 14.9 %all-gather.1 = f32[4096]{0:T(1024)S(1)} all-gather(f32[1024]{0:T(1024)S(1)} %fusion.6), channel_id=3, replica_groups=mesh['tp'=4,'pp'=8] {'tp'}, dimensions={0}, use_global_device_ids=true | all-gather | bytes 20480 | tf_op jit(solution)/shard_map/all_gather | solution.py:51
  26.0 3.8 fusion.8
  29.8 3.6 collective-permute-start
  34.7 85.9 %collective-permute-done = bf16[1024,2048]{1,0:T(8,128)(2,1)S(1)} collective-permute-done((bf16[1024,2048]{1,0:T(8,128)(2,1)S(1)}, bf16[1024,2048]{1,0:T(8,128)(2,1)S(1)}, u32[]{:S(2)}, u32[]{:S(2)}) %collective-permute-start) | collective-permute-done | bytes 4194336 | tf_op jit(solution)/shard_map/ppermute | solution.py:74
  130.9 87.9 %collective-permute-done.3 = bf16[1024,2048]{1,0:T(8,128)(2,1)} collective-permute-done((bf16[1024,2048]{1,0:T(8,128)(2,1)S(1)}, bf16[1024,2048]{1,0:T(8,128)(2,1)}, u32[]{:S(2)}, u32[]{:S(2)}) %collective-permute-start.3) | collective-permute-done | bytes 4194336 | tf_op jit(solution)/shard_map/ppermute | solution.py:75
  227.1 4.6 broadcast_select_fusion.1
  231.7 77.9 %collective-permute-done.5 = bf16[1024,2048]{1,0:T(8,128)(2,1)} collective-permute-done((bf16[1024,2048]{1,0:T(8,128)(2,1)}, bf16[1024,2048]{1,0:T(8,128)(2,1)}, u32[]{:S(2)}, u32[]{:S(2)}) %collective-permute-start.5) | collective-permute-done | bytes 4194336 | tf_op jit(solution)/shard_map/ppermute | solution.py:75
  309.6 4.5 broadcast_select_fusion
  314.2 11.0 %fusion.30 = f32[1024,2,1280]{2,0,1:T(8,128)} fusion(bf16[8,2,1280,1024]{3,2,1,0:T(8,128)(2,1)} %bitcast.199, s32[]{:T(128)S(6)} %select_n.83, bf16[1024,2048]{1,0:T(8,128)(2,1)} %copy-done.5), kind=kOutput, calls=%fused_computation.50 | convolution fusion | flops 5368709120 | bytes 17825796 | tf_op jit(solution)/shard_map/td,grd->tgr/dot_general | solution.py:62
  325.2 12.4 %convolution_add_fusion.5 = f32[1024,2,1280]{2,0,1:T(8,128)} fusion(f32[1024,2,1280]{2,0,1:T(8,128)} %fusion.30, bf16[8,2,1280,1024]{3,2,1,0:T(8,128)(2,1)} %bitcast.200, s32[]{:T(128)S(6)} %select_n.84, bf16[1024,2048]{1,0:T(8,128)(2,1)S(1)} %copy-done.6), kind=kOutput, calls=%fused_computation.28 | convolution fusion | flops 5371330560 | bytes 28311556 | tf_op jit(solution)/shard_map/td,grd->tgr/dot_general | solution.py:62
  337.6 12.3 %convolution_add_fusion.4 = f32[1024,2,1280]{2,0,1:T(8,128)} fusion(f32[1024,2,1280]{2,0,1:T(8,128)} %convolution_add_fusion.5, bf16[8,2,1280,1024]{3,2,1,0:T(8,128)(2,1)} %bitcast.201, s32[]{:T(128)S(6)} %select_n.85, bf16[1024,2048]{1,0:T(8,128)(2,1)S(1)} %copy-done.18), kind=kOutput, calls=%fused_computation.27 | convolution fusion | flops 5371330560 | bytes 28311556 | tf_op jit(solution)/shard_map/td,grd->tgr/dot_general | solution.py:62
  349.9 11.2 %fusion.26 = f32[1024,2,1280]{2,0,1:T(8,128)} fusion(bf16[8,2,1280,1024]{3,2,1,0:T(8,128)(2,1)} %bitcast.202, s32[]{:T(128)S(6)} %select_n.86, bf16[1024,2048]{1,0:T(8,128)(2,1)S(1)} %copy-done.18), kind=kOutput, calls=%fused_computation.46 | convolution fusion | flops 5368709120 | bytes 17825796 | tf_op jit(solution)/shard_map/td,grd->tgr/dot_general | solution.py:62
  361.1 12.1 %add.126 = f32[1024,2,1280]{2,0,1:T(8,128)} add(f32[1024,2,1280]{2,0,1:T(8,128)} %convolution_add_fusion.4, f32[1024,2,1280]{2,0,1:T(8,128)} %fusion.26) | non-fusion elementwise | flops 2621440 | bytes 31457280 | tf_op jit(solution)/shard_map/add | solution.py:68
  373.3 11.1 %fusion.24 = f32[1024,2,1280]{2,0,1:T(8,128)} fusion(bf16[8,2,1280,1024]{3,2,1,0:T(8,128)(2,1)} %bitcast.203, s32[]{:T(128)S(6)} %select_n.87, bf16[1024,2048]{1,0:T(8,128)(2,1)} %copy-done.16), kind=kOutput, calls=%fused_computation.44 | convolution fusion | flops 5368709120 | bytes 17825796 | tf_op jit(solution)/shard_map/td,grd->tgr/dot_general | solution.py:62
  384.3 12.1 %add.129 = f32[1024,2,1280]{2,0,1:T(8,128)} add(f32[1024,2,1280]{2,0,1:T(8,128)} %add.126, f32[1024,2,1280]{2,0,1:T(8,128)} %fusion.24) | non-fusion elementwise | flops 2621440 | bytes 31457280 | tf_op jit(solution)/shard_map/add | solution.py:68
  396.5 11.1 %fusion.22 = f32[1024,2,1280]{2,0,1:T(8,128)} fusion(bf16[8,2,1280,1024]{3,2,1,0:T(8,128)(2,1)} %bitcast.204, s32[]{:T(128)S(6)} %select_n.88, bf16[1024,2048]{1,0:T(8,128)(2,1)} %copy-done.16), kind=kOutput, calls=%fused_computation.42 | convolution fusion | flops 5368709120 | bytes 17825796 | tf_op jit(solution)/shard_map/td,grd->tgr/dot_general | solution.py:62
  407.5 12.1 %add.132 = f32[1024,2,1280]{2,0,1:T(8,128)} add(f32[1024,2,1280]{2,0,1:T(8,128)} %add.129, f32[1024,2,1280]{2,0,1:T(8,128)} %fusion.22) | non-fusion elementwise | flops 2621440 | bytes 31457280 | tf_op jit(solution)/shard_map/add | solution.py:68
  419.7 12.6 %convolution_add_fusion.3 = f32[1024,2,1280]{2,0,1:T(8,128)} fusion(f32[1024,2,1280]{2,0,1:T(8,128)} %add.132, bf16[8,2,1280,1024]{3,2,1,0:T(8,128)(2,1)} %bitcast.205, s32[]{:T(128)S(6)} %select_n.92, bf16[1024,2048]{1,0:T(8,128)(2,1)} %broadcast_select_fusion.1), kind=kOutput, calls=%fused_computation.26 | convolution fusion | flops 5371330560 | bytes 28311556 | tf_op jit(solution)/shard_map/td,grd->tgr/dot_general | solution.py:62
  432.2 12.6 %convolution_add_fusion.2 = f32[1024,2,1280]{2,0,1:T(8,128)} fusion(f32[1024,2,1280]{2,0,1:T(8,128)} %convolution_add_fusion.3, bf16[8,2,1280,1024]{3,2,1,0:T(8,128)(2,1)} %bitcast.206, s32[]{:T(128)S(6)} %select_n.93, bf16[1024,2048]{1,0:T(8,128)(2,1)S(1)} %copy-done.7), kind=kOutput, calls=%fused_computation.25 | convolution fusion | flops 5371330560 | bytes 28311556 | tf_op jit(solution)/shard_map/td,grd->tgr/dot_general | solution.py:62
  444.8 12.3 %convolution_add_fusion.1 = f32[1024,2,1280]{2,0,1:T(8,128)} fusion(f32[1024,2,1280]{2,0,1:T(8,128)} %convolution_add_fusion.2, bf16[8,2,1280,1024]{3,2,1,0:T(8,128)(2,1)} %bitcast.207, s32[]{:T(128)S(6)} %select_n.97, bf16[1024,2048]{1,0:T(8,128)(2,1)S(1)} %copy-done.8), kind=kOutput, calls=%fused_computation.24 | convolution fusion | flops 5371330560 | bytes 28311556 | tf_op jit(solution)/shard_map/td,grd->tgr/dot_general | solution.py:62
  457.1 12.3 %convolution_add_fusion = f32[1024,2,1280]{2,0,1:T(8,128)} fusion(f32[1024,2,1280]{2,0,1:T(8,128)} %convolution_add_fusion.1, bf16[8,2,1280,1024]{3,2,1,0:T(8,128)(2,1)} %bitcast.208, s32[]{:T(128)S(6)} %select_n.98, bf16[1024,2048]{1,0:T(8,128)(2,1)S(1)} %copy-done.8), kind=kOutput, calls=%fused_computation.23 | convolution fusion | flops 5371330560 | bytes 28311556 | tf_op jit(solution)/shard_map/td,grd->tgr/dot_general | solution.py:62
  469.4 11.3 %copy.48 = f32[1024,2,1280]{0,2,1:T(8,128)} copy(f32[1024,2,1280]{2,0,1:T(8,128)} %convolution_add_fusion) | data formatting | bytes 20971520 | tf_op jit(solution)/shard_map/optimization_barrier | solution.py:68
  480.6 8.6 %fusion.114 = (f32[1024,2,8,64]{0,3,2,1:T(8,128)}, f32[1024,2,8,64]{0,3,2,1:T(8,128)}) fusion(f32[1024,2,10,128]{0,3,2,1:T(8,128)} %bitcast.190), kind=kLoop, calls=%fused_computation.161 | loop fusion | bytes 16777216 | tf_op jit(solution)/shard_map/slice | solution.py:29
  492.5 6.9 %copy.74 = f32[1024,2,8,64]{3,0,2,1:T(8,128)} copy(f32[1024,2,8,64]{0,3,2,1:T(8,128)} %get-tuple-element.7) | data formatting | bytes 8388608
  499.4 6.9 %copy.75 = f32[1024,2,8,64]{3,0,2,1:T(8,128)} copy(f32[1024,2,8,64]{0,3,2,1:T(8,128)} %get-tuple-element.6) | data formatting | bytes 8388608
  507.1 7.3 %subtract_convert_fusion = (bf16[1024,2,8,64]{3,0,2,1:T(8,128)(2,1)S(1)}, bf16[1024,2,8,64]{3,0,2,1:T(8,128)(2,1)S(1)}) fusion(f32[1024,2,8,64]{3,0,2,1:T(8,128)} %copy.75, f32[1024,2,8,64]{3,0,2,1:T(8,128)} %copy.74, f32[1024,64]{1,0:T(8,128)S(1)} %copy-done.4, f32[1024,64]{1,0:T(8,128)S(1)} %copy-done.3), kind=kLoop, calls=%fused_computation.22 | loop fusion | flops 8388608 | bytes 13107200 | tf_op jit(solution)/shard_map/convert
  517.8 4.5 fusion.64
  525.9 9.6 %fusion.130 = (f32[2,8,256]{2,1,0:T(8,128)S(1)}, f32[2,8,256,512]{2,3,1,0:T(8,128)S(1)}) fusion(f32[2,512,256,8]{2,1,3,0:T(8,128)} %fusion.64, pred[256,512]{0,1:T(8,128)(4,1)S(1)} %copy-done.12), kind=kOutput, calls=%fused_computation.165 | output fusion | flops 14680575 | bytes 16924672 | tf_op jit(solution)/shard_map/sub | solution.py:106
  540.0 11.5 %fusion.121 = (f32[2,8,256]{2,1,0:T(8,128)S(1)}, f32[2,8,256,768]{2,3,1,0:T(8,128)}) fusion(pred[256,768]{0,1:T(8,128)(4,1)S(1)} %copy-done.11, bf16[1024,2,64]{2,0,1:T(8,128)(2,1)S(1)} %get-tuple-element.8, bf16[1024,2,64]{2,0,1:T(8,128)(2,1)S(1)} %get-tuple-element.9, bf16[1024,2,8,64]{3,0,2,1:T(8,128)(2,1)} %copy-done.1, ...), kind=kOutput, calls=%fused_computation.164 | convolution fusion | flops 823919360 | bytes 18235392 | tf_op jit(solution)/shard_map/sub | solution.py:106
  551.5 6.8 %fusion.54 = bf16[2,128,8,256]{3,1,2,0:T(8,128)(2,1)} fusion(f32[2,8,256,768]{2,3,1,0:T(8,128)} %get-tuple-element.19, f32[2,8,256]{2,1,0:T(8,128)S(1)} %get-tuple-element.18, bf16[1024,2,10,128]{0,3,1,2:T(8,128)(2,1)} %copy.78), kind=kOutput, calls=%fused_computation.98 | convolution fusion | flops 812122112 | bytes 14041088 | tf_op jit(solution)/shard_map/gjts,sgd->tgjd/dot_general | solution.py:108
  560.8 11.5 %fusion.116 = (f32[2,8,256]{2,1,0:T(8,128)S(1)}, f32[2,8,256,768]{2,3,1,0:T(8,128)}) fusion(pred[256,768]{0,1:T(8,128)(4,1)S(1)} %copy-done.10, bf16[1024,2,64]{2,0,1:T(8,128)(2,1)S(1)} %get-tuple-element.9, bf16[1024,2,64]{2,0,1:T(8,128)(2,1)S(1)} %get-tuple-element.8, bf16[1024,2,8,64]{3,0,2,1:T(8,128)(2,1)} %copy-done.2, ...), kind=kOutput, calls=%fused_computation.163 | convolution fusion | flops 823919360 | bytes 17514496 | tf_op jit(solution)/shard_map/sub | solution.py:106
  572.4 6.7 %fusion.53 = bf16[2,128,8,256]{3,1,2,0:T(8,128)(2,1)} fusion(f32[2,8,256,768]{2,3,1,0:T(8,128)} %get-tuple-element.17, f32[2,8,256]{2,1,0:T(8,128)S(1)} %get-tuple-element.16, bf16[1024,2,10,128]{0,3,1,2:T(8,128)(2,1)} %copy.78), kind=kOutput, calls=%fused_computation.97 | convolution fusion | flops 812122112 | bytes 14041088 | tf_op jit(solution)/shard_map/gjts,sgd->tgjd/dot_general | solution.py:108
  (89 shorter events, 51.7 us)
Async XLA Ops:
  7.2 18.8 %copy-start.15 = (bf16[2048]{0:T(1024)(128)(2,1)S(1)}, bf16[2048]{0:T(1024)(128)(2,1)}, u32[]{:S(2)}) copy-start(bf16[2048]{0:T(1024)(128)(2,1)} %param.5) | copy-start | bytes 12292
  7.2 307.0 %all-gather.4.cloned.1.call-start = ((), (), s32[]{:S(2)}) async-start(), calls=%async_computation | async-start | bytes 47185920 | tf_op jit(solution)/shard_map/all_gather | solution.py:43
  11.0 209.2 %copy-start.13 = (s32[1,1024]{1,0:T(1,128)S(1)}, s32[1,1024]{1,0:T(1,128)}, u32[]{:S(2)}) copy-start(s32[1,1024]{1,0:T(1,128)} %param.7) | copy-start | bytes 12292
  29.8 3.6 copy-start.5
  29.8 90.8 %collective-permute-start = (bf16[1024,2048]{1,0:T(8,128)(2,1)S(1)}, bf16[1024,2048]{1,0:T(8,128)(2,1)S(1)}, u32[]{:S(2)}, u32[]{:S(2)}) collective-permute-start(bf16[1024,2048]{1,0:T(8,128)(2,1)S(1)} %fusion.8), channel_id=1, source_target_pairs={{0,8},{8,16},{16,24},{1,9},{9,17},{17,25},{2,10},{10,18},{18,26},{... | collective-permute-start | bytes 12582920 | tf_op jit(solution)/shard_map/ppermute | solution.py:74
  33.4 91.6 %collective-permute-start.1 = (bf16[1024,2048]{1,0:T(8,128)(2,1)S(1)}, bf16[1024,2048]{1,0:T(8,128)(2,1)S(1)}, u32[]{:S(2)}, u32[]{:S(2)}) collective-permute-start(bf16[1024,2048]{1,0:T(8,128)(2,1)S(1)} %fusion.8), channel_id=1, source_target_pairs={{8,0},{16,8},{24,16},{9,1},{17,9},{25,17},{10,2},{18,10},{26,18},{... | collective-permute-start | bytes 12582920 | tf_op jit(solution)/shard_map/ppermute | solution.py:75
  120.6 98.2 %copy-start.17 = (bf16[1024,2048]{1,0:T(8,128)(2,1)}, bf16[1024,2048]{1,0:T(8,128)(2,1)S(1)}, u32[]{:S(2)}) copy-start(bf16[1024,2048]{1,0:T(8,128)(2,1)S(1)} %collective-permute-done) | copy-start | bytes 12582916
  120.6 7.6 %collective-permute-start.2 = (bf16[1024,2048]{1,0:T(8,128)(2,1)S(1)}, bf16[1024,2048]{1,0:T(8,128)(2,1)}, u32[]{:S(2)}, u32[]{:S(2)}) collective-permute-start(bf16[1024,2048]{1,0:T(8,128)(2,1)S(1)} %collective-permute-done), channel_id=1, source_target_pairs={{8,16},{16,24},{9,17},{17,25},{10,18},{18,26},{11,19},{19,27},{12,... | collective-permute-start | bytes 12582920 | tf_op jit(solution)/shard_map/ppermute | solution.py:74
  125.0 1.9 copy-start.16
  126.9 91.8 %collective-permute-start.3 = (bf16[1024,2048]{1,0:T(8,128)(2,1)S(1)}, bf16[1024,2048]{1,0:T(8,128)(2,1)}, u32[]{:S(2)}, u32[]{:S(2)}) collective-permute-start(bf16[1024,2048]{1,0:T(8,128)(2,1)S(1)} %collective-permute-done.1), channel_id=1, source_target_pairs={{8,0},{16,8},{9,1},{17,9},{10,2},{18,10},{11,3},{19,11},{12,4},{20... | collective-permute-start | bytes 12582920 | tf_op jit(solution)/shard_map/ppermute | solution.py:75
  128.2 103.5 %collective-permute-start.4 = (bf16[1024,2048]{1,0:T(8,128)(2,1)}, bf16[1024,2048]{1,0:T(8,128)(2,1)}, u32[]{:S(2)}, u32[]{:S(2)}) collective-permute-start(bf16[1024,2048]{1,0:T(8,128)(2,1)} %collective-permute-done.2), channel_id=1, source_target_pairs={{16,24},{17,25},{18,26},{19,27},{20,28},{21,29},{22,30},{23,31}} | collective-permute-start | bytes 12582920 | tf_op jit(solution)/shard_map/ppermute | solution.py:74
  218.8 90.8 %collective-permute-start.5 = (bf16[1024,2048]{1,0:T(8,128)(2,1)}, bf16[1024,2048]{1,0:T(8,128)(2,1)}, u32[]{:S(2)}, u32[]{:S(2)}) collective-permute-start(bf16[1024,2048]{1,0:T(8,128)(2,1)} %collective-permute-done.3), channel_id=1, source_target_pairs={{8,0},{9,1},{10,2},{11,3},{12,4},{13,5},{14,6},{15,7}} | collective-permute-start | bytes 12582920 | tf_op jit(solution)/shard_map/ppermute | solution.py:75
  314.2 11.1 %copy-start.6 = (bf16[1024,2048]{1,0:T(8,128)(2,1)S(1)}, bf16[1024,2048]{1,0:T(8,128)(2,1)}, u32[]{:S(2)}) copy-start(bf16[1024,2048]{1,0:T(8,128)(2,1)} %copy-done.5) | copy-start | bytes 12582916
  325.2 12.4 %copy-start.18 = (bf16[1024,2048]{1,0:T(8,128)(2,1)S(1)}, bf16[1024,2048]{1,0:T(8,128)(2,1)}, u32[]{:S(2)}) copy-start(bf16[1024,2048]{1,0:T(8,128)(2,1)} %copy-done.17) | copy-start | bytes 12582916
  419.7 12.6 %copy-start.7 = (bf16[1024,2048]{1,0:T(8,128)(2,1)S(1)}, bf16[1024,2048]{1,0:T(8,128)(2,1)}, u32[]{:S(2)}) copy-start(bf16[1024,2048]{1,0:T(8,128)(2,1)} %broadcast_select_fusion.1) | copy-start | bytes 12582916
  432.2 12.6 %copy-start.8 = (bf16[1024,2048]{1,0:T(8,128)(2,1)S(1)}, bf16[1024,2048]{1,0:T(8,128)(2,1)}, u32[]{:S(2)}) copy-start(bf16[1024,2048]{1,0:T(8,128)(2,1)} %broadcast_select_fusion) | copy-start | bytes 12582916
  480.6 8.6 %copy-start = (f32[1024,2,1280]{0,2,1:T(8,128)S(1)}, f32[1024,2,1280]{0,2,1:T(8,128)}, u32[]{:S(2)}) copy-start(f32[1024,2,1280]{0,2,1:T(8,128)} %copy.48) | copy-start | bytes 31457284
  499.4 7.3 %copy-start.3 = (f32[1024,64]{1,0:T(8,128)S(1)}, f32[1024,64]{1,0:T(8,128)}, u32[]{:S(2)}) copy-start(f32[1024,64]{1,0:T(8,128)} %get-tuple-element.10) | copy-start | bytes 786436
  499.4 7.3 %copy-start.4 = (f32[1024,64]{1,0:T(8,128)S(1)}, f32[1024,64]{1,0:T(8,128)}, u32[]{:S(2)}) copy-start(f32[1024,64]{1,0:T(8,128)} %get-tuple-element.11) | copy-start | bytes 786436
  514.4 2.0 copy-start.1
  514.5 3.4 copy-start.2
  517.8 4.6 copy-start.14
  523.8 2.1 copy-start.12
  535.5 4.5 copy-start.11
  551.5 9.3 %copy-start.10 = (pred[256,768]{0,1:T(8,128)(4,1)S(1)}, pred[256,768]{0,1:T(8,128)(4,1)}, u32[]{:S(2)}) copy-start(pred[256,768]{0,1:T(8,128)(4,1)} %get-tuple-element.24) | copy-start | bytes 589828
  584.0 3.2 copy-start.9
Sparse Core Ops, SparseCore 0:
  9.9 199.7 all-gather.3
